TPU v7x, 32 devices: a whole 2x2x4 slice. The times are simulated.
32 devices in a mesh: grp: 2 (over x), seq: 16 (over z, y, core).
Axes of the slice: x: 2, y: 2, z: 4, core: 2. Of those that a mesh axis runs over, the one named last changes fastest.
Arguments:
- queries: bfloat16 [16384, 4096], P(('grp', 'seq')), parts along dimension 0, may hold values from -40 to 40
- kv_cache: bfloat16 [2, 16384, 1024], P(None, ('grp', 'seq')), parts along dimension 1, may hold values from -4 to 4
- question: bfloat16 [64, 4096], P('grp'), parts along dimension 0, may hold values from -40 to 40
Outputs:
- context_out: bfloat16 [16384, 4096], P(('grp', 'seq')), parts along dimension 0
- answer: bfloat16 [64, 4096], P(('grp', 'seq')), parts along dimension 0
There are 2 independent parts, one for each index of `grp`. A program takes and returns all parts, laid end to end along the dimension named above; each array names one. Nothing has to cross between parts.
All inputs are finite; a program needn't handle non-finite values.
Results may differ from a plain program's by a relative error of at most 0.004.
Values may be sent and summed in bfloat16 or wider, within the bound.
A program may use at most 256 MiB of HBM per device.

v0:
```python
import jax
import jax.numpy as jnp
from jax import lax
from jax.sharding import PartitionSpec as P

HEAD = 128


big_negative = -1e30


def from_root(x, axis, root):
    mine = lax.axis_index(axis) == root
    return lax.psum(jnp.where(mine, x, jnp.zeros_like(x)), axis)


def combined_all(x, axis, combine):
    everything = jax.tree.map(lambda part: lax.all_gather(part, axis), x)
    first = jax.tree.map(lambda part: part[0], everything)

    def turn(k, so_far):
        return combine(so_far, jax.tree.map(lambda part: part[k], everything))

    return lax.fori_loop(1, lax.axis_size(axis), turn, first)


def group_split(rows_in, groups):
    row_count = rows_in.shape[0]
    return rows_in.reshape(row_count, groups, rows_in.shape[1] // groups).transpose(1, 0, 2)


def visible(block_number, row_count, anchor_rows):
    row_pos = lax.broadcasted_iota(jnp.int32, (row_count, anchor_rows + row_count), 0)
    column = lax.broadcasted_iota(jnp.int32, (row_count, anchor_rows + row_count), 1)
    return jnp.where(column < anchor_rows, block_number > 0, column - anchor_rows <= row_pos)


def block_attention(rows_q, keys_all, values_all, allowed):
    groups = keys_all.shape[1] // HEAD
    group_ratio = rows_q.shape[1] // keys_all.shape[1]
    score_scale = HEAD ** (-0.5)

    def one_group(pieces):
        query_part, key_part, value_part = pieces
        query_part = query_part.reshape(query_part.shape[0], group_ratio, HEAD)
        scores = (
            jnp.einsum("brd,kd->rbk", query_part, key_part, preferred_element_type=jnp.float32)
            * score_scale
        )
        scores = jnp.where(allowed[None], scores, big_negative)
        highest = jnp.max(scores, axis=2, keepdims=True)
        exponent = jnp.exp(scores - highest)
        totals = jnp.sum(exponent, axis=2)
        soft_weights = exponent.astype(jnp.bfloat16)
        mixture = jnp.einsum(
            "rbk,kd->brd", soft_weights, value_part, preferred_element_type=jnp.float32
        )
        mixture = mixture / totals.T[:, :, None]
        return mixture.astype(jnp.bfloat16).reshape(mixture.shape[0], group_ratio * HEAD)

    result = lax.map(
        one_group,
        (
            group_split(rows_q, groups),
            group_split(keys_all, groups),
            group_split(values_all, groups),
        ),
    )
    return result.transpose(1, 0, 2).reshape(rows_q.shape[0], rows_q.shape[1])


def block_summary(rows_q, key_block, value_block):
    groups = key_block.shape[1] // HEAD
    group_ratio = rows_q.shape[1] // key_block.shape[1]
    score_scale = HEAD ** (-0.5)
    row_count = rows_q.shape[0]

    def one_group(pieces):
        query_part, key_part, value_part = pieces
        query_part = query_part.reshape(row_count, group_ratio, HEAD)
        scores = (
            jnp.einsum("qrd,kd->rqk", query_part, key_part, preferred_element_type=jnp.float32)
            * score_scale
        )
        highest = jnp.max(scores, axis=2)
        exponent = jnp.exp(scores - highest[:, :, None])
        totals = jnp.sum(exponent, axis=2)
        soft_weights = exponent.astype(jnp.bfloat16)
        mixture = jnp.einsum(
            "rqk,kd->qrd", soft_weights, value_part, preferred_element_type=jnp.float32
        )
        return (highest.T, totals.T, mixture)

    highs, totals, mixture = lax.map(
        one_group,
        (
            group_split(rows_q, groups),
            group_split(key_block, groups),
            group_split(value_block, groups),
        ),
    )
    highs = highs.transpose(1, 0, 2).reshape(row_count, groups * group_ratio)
    totals = totals.transpose(1, 0, 2).reshape(row_count, groups * group_ratio)
    mixture = mixture.transpose(1, 0, 2, 3).reshape(row_count, groups * group_ratio, HEAD)
    return (highs, totals, mixture)


def combine(former, latter):
    highest = jnp.maximum(former[0], latter[0])
    factor_former = jnp.exp(former[0] - highest)
    factor_latter = jnp.exp(latter[0] - highest)
    totals = former[1] * factor_former + latter[1] * factor_latter
    mixture = former[2] * factor_former[..., None] + latter[2] * factor_latter[..., None]
    return (highest, totals, mixture)


def on_device(queries, kv_cache, question):
    dev_index = lax.axis_index("seq")
    anchor = from_root(kv_cache, "seq", 0)
    row_count = queries.shape[0]
    keys_all = jnp.concatenate((anchor[0], kv_cache[0]), axis=0)
    values_all = jnp.concatenate((anchor[1], kv_cache[1]), axis=0)
    allowed = visible(dev_index, row_count, anchor.shape[1])
    context_out = block_attention(queries, keys_all, values_all, allowed)
    highs, totals, mixture = block_summary(question, kv_cache[0], kv_cache[1])
    highest, den_all, num_all = combined_all((highs, totals, mixture), "seq", combine)
    row_share = den_all.shape[0] // lax.axis_size("seq")
    row_start = dev_index * row_share
    denominator = lax.dynamic_slice_in_dim(den_all, row_start, row_share, 0)
    numerator = lax.dynamic_slice_in_dim(num_all, row_start, row_share, 0)
    answer = (numerator / denominator[..., None]).astype(jnp.bfloat16)
    answer = answer.reshape(numerator.shape[0], question.shape[1])
    return (context_out, answer)


def solution(mesh):
    return jax.shard_map(
        on_device,
        mesh=mesh,
        in_specs=(P(("grp", "seq"), None), P(None, ("grp", "seq"), None), P("grp", None)),
        out_specs=(P(("grp", "seq"), None), P(("grp", "seq"), None)),
        check_vma=False,
    )
```

profile of v0, /device:TPU:24, one launch (start us, length us, event | category | flops | bytes accessed | tf_op | source)
XLA Modules:
  0.0 239.3 jit_solution(4618223693420680374)
XLA Ops:
  7.2 2.9 %copy.33 = bf16[2,512,1024]{1,2,0:T(8,128)(2,1)S(1)} copy(bf16[2,512,1024]{2,1,0:T(8,128)(2,1)} %param.10) | data formatting | bytes 4194304 | tf_op args[1]
  13.8 11.2 %while.44 = (s32[]{:T(128)}, f32[8,32,4]{1,2,0:T(4,128)S(1)}, f32[8,32,4]{1,2,0:T(4,128)S(1)}, f32[8,32,4,128]{3,1,2,0:T(8,128)}, bf16[8,512,128]{1,2,0:T(8,128)...) while((s32[]{:T(128)}, f32[8,32,4]{1,2,0:T(4,128)S(1)}, ...), condition=%wide.region_8.9_spmd, body=%wide.region_5.8_spmd.sunk | while | flops 33947392 | bytes 1290849 | solution.py:94
  25.0 2.2 copy.44
  27.3 17.8 %all_gather.10 = f32[16,32,32]{2,1,0:T(8,128)S(1)} all-gather(f32[1,32,32]{2,1,0:T(8,128)S(1)} %copy.43), channel_id=1, replica_groups=mesh['grp'=2,'seq'=16] {'seq'}, dimensions={0}, use_global_device_ids=true | all-gather | bytes 69632 | tf_op jit(solution)/shard_map/all_gather | solution.py:18
  45.2 19.2 %all_gather.9 = f32[16,32,32]{2,1,0:T(8,128)S(1)} all-gather(f32[1,32,32]{2,1,0:T(8,128)S(1)} %copy.42), channel_id=1, replica_groups=mesh['grp'=2,'seq'=16] {'seq'}, dimensions={0}, use_global_device_ids=true | all-gather | bytes 69632 | tf_op jit(solution)/shard_map/all_gather | solution.py:18
  64.4 6.4 %copy.36 = bf16[512,4096]{0,1:T(8,128)(2,1)} copy(bf16[512,4096]{1,0:T(8,128)(2,1)} %param.9) | data formatting | bytes 8388608 | tf_op args[0]
  70.8 40.4 %all-reduce.2.cloned.1.call-done = bf16[2,512,1024]{1,2,0:T(8,128)(2,1)} async-done(((bf16[2,512,1024]{1,2,0:T(8,128)(2,1)}), bf16[2,512,1024]{1,2,0:T(8,128)(2,1)}) %all-reduce.2.cloned.1.call-update) | async-done | bytes 2097168 | tf_op jit(solution)/shard_map/psum | solution.py:14
  111.1 1.7 fusion.42
  112.8 2.5 %maximum_bitcast_fusion = (bf16[8,1024,128]{1,2,0:T(8,128)(2,1)}, bf16[8,1024,128]{1,2,0:T(8,128)(2,1)}) fusion(bf16[512,8,128]{0,2,1:T(8,128)(2,1)S(1)} %bitcast.152, bf16[512,8,128]{0,2,1:T(8,128)(2,1)S(1)} %bitcast.156, bf16[512,8,128]{0,2,1:T(8,128)(2,1)S(1)} %bitcast.154, bf16[512,8,128]{0,2,1:T(8,128)(2,1)S(1)} %bitcast.155), kind=kLoop, calls=%fused_computation.49 | loop fusion | flops 8388608 | bytes 8388608 | tf_op jit(solution)/shard_map/transpose | solution.py:29
  115.3 85.0 %while.46 = (s32[]{:T(128)}, bf16[8,512,512]{1,2,0:T(8,128)(2,1)}, bf16[8,1024,128]{1,2,0:T(8,128)(2,1)}, bf16[8,1024,128]{1,2,0:T(8,128)(2,1)}, bf16[8,512,512]...) while((s32[]{:T(128)}, bf16[8,512,512]{1,2,0:T(8,128)(2,1)}, ...), condition=%wide.region_4.5_spmd.clone, body=%wide.region_1.4_spmd.clone.sunk | while | flops 1098379264 | bytes 30980704 | solution.py:61
  117.3 2.6 %fusion.68 = (f32[4,512]{1,0:T(4,128)S(1)}, f32[1024,512,4]{1,0,2:T(8,128)S(1)}) fusion(pred[512,1024]{0,1:T(8,128)(4,1)S(1)} %fusion.67, bf16[512,4,128]{0,2,1:T(8,128)(2,1)S(1)} %bitcast.148, bf16[8,1024,128]{1,2,0:T(8,128)(2,1)} %get-tuple-element.555, s32[]{:T(128)} %get-tuple-element.543), kind=kOutput, calls=%fused_computation.31.clone.1 | convolution fusion | flops 543160320 | bytes 9708032 | tf_op jit(solution)/shard_map/while/body/eval_jaxpr/brd,kd->rbk/dot_general | solution.py:47
  119.8 1.8 fusion.69
  121.7 3.4 %divide_convert_fusion.3 = bf16[512,4,128]{0,2,1:T(8,128)(2,1)S(1)} fusion(f32[1024,512,4]{1,0,2:T(8,128)S(1)} %get-tuple-element.532, f32[4,512]{1,0:T(4,128)S(1)} %get-tuple-element.533, pred[512,1024]{0,1:T(8,128)(4,1)S(1)} %fusion.67, f32[512,4]{0,1:T(4,128)S(1)} %bitcast.161, bf16[8,1024,128]{1,2,0:T(8,128)(2,1)} %get-tuple-element.554, ...), kind=kOutput, calls=%fused_computation.37.clone.1 | convolution fusion | flops 545783808 | bytes 9716224 | tf_op jit(solution)/shard_map/while/body/eval_jaxpr/rbk,kd->brd/dot_general | solution.py:55
  127.9 2.6 %fusion.68 = (f32[4,512]{1,0:T(4,128)S(1)}, f32[1024,512,4]{1,0,2:T(8,128)S(1)}) fusion(pred[512,1024]{0,1:T(8,128)(4,1)S(1)} %fusion.67, bf16[512,4,128]{0,2,1:T(8,128)(2,1)S(1)} %bitcast.148, bf16[8,1024,128]{1,2,0:T(8,128)(2,1)} %get-tuple-element.555, s32[]{:T(128)} %get-tuple-element.543), kind=kOutput, calls=%fused_computation.31.clone.1 | convolution fusion | flops 543160320 | bytes 9708032 | tf_op jit(solution)/shard_map/while/body/eval_jaxpr/brd,kd->rbk/dot_general | solution.py:47
  130.5 1.8 fusion.69
  132.4 3.4 %divide_convert_fusion.3 = bf16[512,4,128]{0,2,1:T(8,128)(2,1)S(1)} fusion(f32[1024,512,4]{1,0,2:T(8,128)S(1)} %get-tuple-element.532, f32[4,512]{1,0:T(4,128)S(1)} %get-tuple-element.533, pred[512,1024]{0,1:T(8,128)(4,1)S(1)} %fusion.67, f32[512,4]{0,1:T(4,128)S(1)} %bitcast.161, bf16[8,1024,128]{1,2,0:T(8,128)(2,1)} %get-tuple-element.554, ...), kind=kOutput, calls=%fused_computation.37.clone.1 | convolution fusion | flops 545783808 | bytes 9716224 | tf_op jit(solution)/shard_map/while/body/eval_jaxpr/rbk,kd->brd/dot_general | solution.py:55
  138.6 2.6 %fusion.68 = (f32[4,512]{1,0:T(4,128)S(1)}, f32[1024,512,4]{1,0,2:T(8,128)S(1)}) fusion(pred[512,1024]{0,1:T(8,128)(4,1)S(1)} %fusion.67, bf16[512,4,128]{0,2,1:T(8,128)(2,1)S(1)} %bitcast.148, bf16[8,1024,128]{1,2,0:T(8,128)(2,1)} %get-tuple-element.555, s32[]{:T(128)} %get-tuple-element.543), kind=kOutput, calls=%fused_computation.31.clone.1 | convolution fusion | flops 543160320 | bytes 9708032 | tf_op jit(solution)/shard_map/while/body/eval_jaxpr/brd,kd->rbk/dot_general | solution.py:47
  141.1 1.8 fusion.69
  143.0 3.4 %divide_convert_fusion.3 = bf16[512,4,128]{0,2,1:T(8,128)(2,1)S(1)} fusion(f32[1024,512,4]{1,0,2:T(8,128)S(1)} %get-tuple-element.532, f32[4,512]{1,0:T(4,128)S(1)} %get-tuple-element.533, pred[512,1024]{0,1:T(8,128)(4,1)S(1)} %fusion.67, f32[512,4]{0,1:T(4,128)S(1)} %bitcast.161, bf16[8,1024,128]{1,2,0:T(8,128)(2,1)} %get-tuple-element.554, ...), kind=kOutput, calls=%fused_computation.37.clone.1 | convolution fusion | flops 545783808 | bytes 9716224 | tf_op jit(solution)/shard_map/while/body/eval_jaxpr/rbk,kd->brd/dot_general | solution.py:55
  149.3 2.6 %fusion.68 = (f32[4,512]{1,0:T(4,128)S(1)}, f32[1024,512,4]{1,0,2:T(8,128)S(1)}) fusion(pred[512,1024]{0,1:T(8,128)(4,1)S(1)} %fusion.67, bf16[512,4,128]{0,2,1:T(8,128)(2,1)S(1)} %bitcast.148, bf16[8,1024,128]{1,2,0:T(8,128)(2,1)} %get-tuple-element.555, s32[]{:T(128)} %get-tuple-element.543), kind=kOutput, calls=%fused_computation.31.clone.1 | convolution fusion | flops 543160320 | bytes 9708032 | tf_op jit(solution)/shard_map/while/body/eval_jaxpr/brd,kd->rbk/dot_general | solution.py:47
  151.9 1.8 fusion.69
  153.8 3.4 %divide_convert_fusion.3 = bf16[512,4,128]{0,2,1:T(8,128)(2,1)S(1)} fusion(f32[1024,512,4]{1,0,2:T(8,128)S(1)} %get-tuple-element.532, f32[4,512]{1,0:T(4,128)S(1)} %get-tuple-element.533, pred[512,1024]{0,1:T(8,128)(4,1)S(1)} %fusion.67, f32[512,4]{0,1:T(4,128)S(1)} %bitcast.161, bf16[8,1024,128]{1,2,0:T(8,128)(2,1)} %get-tuple-element.554, ...), kind=kOutput, calls=%fused_computation.37.clone.1 | convolution fusion | flops 545783808 | bytes 9716224 | tf_op jit(solution)/shard_map/while/body/eval_jaxpr/rbk,kd->brd/dot_general | solution.py:55
  159.9 2.6 %fusion.68 = (f32[4,512]{1,0:T(4,128)S(1)}, f32[1024,512,4]{1,0,2:T(8,128)S(1)}) fusion(pred[512,1024]{0,1:T(8,128)(4,1)S(1)} %fusion.67, bf16[512,4,128]{0,2,1:T(8,128)(2,1)S(1)} %bitcast.148, bf16[8,1024,128]{1,2,0:T(8,128)(2,1)} %get-tuple-element.555, s32[]{:T(128)} %get-tuple-element.543), kind=kOutput, calls=%fused_computation.31.clone.1 | convolution fusion | flops 543160320 | bytes 9708032 | tf_op jit(solution)/shard_map/while/body/eval_jaxpr/brd,kd->rbk/dot_general | solution.py:47
  162.5 1.8 fusion.69
  164.3 3.4 %divide_convert_fusion.3 = bf16[512,4,128]{0,2,1:T(8,128)(2,1)S(1)} fusion(f32[1024,512,4]{1,0,2:T(8,128)S(1)} %get-tuple-element.532, f32[4,512]{1,0:T(4,128)S(1)} %get-tuple-element.533, pred[512,1024]{0,1:T(8,128)(4,1)S(1)} %fusion.67, f32[512,4]{0,1:T(4,128)S(1)} %bitcast.161, bf16[8,1024,128]{1,2,0:T(8,128)(2,1)} %get-tuple-element.554, ...), kind=kOutput, calls=%fused_computation.37.clone.1 | convolution fusion | flops 545783808 | bytes 9716224 | tf_op jit(solution)/shard_map/while/body/eval_jaxpr/rbk,kd->brd/dot_general | solution.py:55
  170.5 2.6 %fusion.68 = (f32[4,512]{1,0:T(4,128)S(1)}, f32[1024,512,4]{1,0,2:T(8,128)S(1)}) fusion(pred[512,1024]{0,1:T(8,128)(4,1)S(1)} %fusion.67, bf16[512,4,128]{0,2,1:T(8,128)(2,1)S(1)} %bitcast.148, bf16[8,1024,128]{1,2,0:T(8,128)(2,1)} %get-tuple-element.555, s32[]{:T(128)} %get-tuple-element.543), kind=kOutput, calls=%fused_computation.31.clone.1 | convolution fusion | flops 543160320 | bytes 9708032 | tf_op jit(solution)/shard_map/while/body/eval_jaxpr/brd,kd->rbk/dot_general | solution.py:47
  173.1 1.8 fusion.69
  175.0 3.4 %divide_convert_fusion.3 = bf16[512,4,128]{0,2,1:T(8,128)(2,1)S(1)} fusion(f32[1024,512,4]{1,0,2:T(8,128)S(1)} %get-tuple-element.532, f32[4,512]{1,0:T(4,128)S(1)} %get-tuple-element.533, pred[512,1024]{0,1:T(8,128)(4,1)S(1)} %fusion.67, f32[512,4]{0,1:T(4,128)S(1)} %bitcast.161, bf16[8,1024,128]{1,2,0:T(8,128)(2,1)} %get-tuple-element.554, ...), kind=kOutput, calls=%fused_computation.37.clone.1 | convolution fusion | flops 545783808 | bytes 9716224 | tf_op jit(solution)/shard_map/while/body/eval_jaxpr/rbk,kd->brd/dot_general | solution.py:55
  181.1 2.6 %fusion.68 = (f32[4,512]{1,0:T(4,128)S(1)}, f32[1024,512,4]{1,0,2:T(8,128)S(1)}) fusion(pred[512,1024]{0,1:T(8,128)(4,1)S(1)} %fusion.67, bf16[512,4,128]{0,2,1:T(8,128)(2,1)S(1)} %bitcast.148, bf16[8,1024,128]{1,2,0:T(8,128)(2,1)} %get-tuple-element.555, s32[]{:T(128)} %get-tuple-element.543), kind=kOutput, calls=%fused_computation.31.clone.1 | convolution fusion | flops 543160320 | bytes 9708032 | tf_op jit(solution)/shard_map/while/body/eval_jaxpr/brd,kd->rbk/dot_general | solution.py:47
  183.7 1.8 fusion.69
  185.5 3.4 %divide_convert_fusion.3 = bf16[512,4,128]{0,2,1:T(8,128)(2,1)S(1)} fusion(f32[1024,512,4]{1,0,2:T(8,128)S(1)} %get-tuple-element.532, f32[4,512]{1,0:T(4,128)S(1)} %get-tuple-element.533, pred[512,1024]{0,1:T(8,128)(4,1)S(1)} %fusion.67, f32[512,4]{0,1:T(4,128)S(1)} %bitcast.161, bf16[8,1024,128]{1,2,0:T(8,128)(2,1)} %get-tuple-element.554, ...), kind=kOutput, calls=%fused_computation.37.clone.1 | convolution fusion | flops 545783808 | bytes 9716224 | tf_op jit(solution)/shard_map/while/body/eval_jaxpr/rbk,kd->brd/dot_general | solution.py:55
  191.7 2.6 %fusion.68 = (f32[4,512]{1,0:T(4,128)S(1)}, f32[1024,512,4]{1,0,2:T(8,128)S(1)}) fusion(pred[512,1024]{0,1:T(8,128)(4,1)S(1)} %fusion.67, bf16[512,4,128]{0,2,1:T(8,128)(2,1)S(1)} %bitcast.148, bf16[8,1024,128]{1,2,0:T(8,128)(2,1)} %get-tuple-element.555, s32[]{:T(128)} %get-tuple-element.543), kind=kOutput, calls=%fused_computation.31.clone.1 | convolution fusion | flops 543160320 | bytes 9708032 | tf_op jit(solution)/shard_map/while/body/eval_jaxpr/brd,kd->rbk/dot_general | solution.py:47
  194.3 1.8 fusion.69
  196.1 3.4 %divide_convert_fusion.3 = bf16[512,4,128]{0,2,1:T(8,128)(2,1)S(1)} fusion(f32[1024,512,4]{1,0,2:T(8,128)S(1)} %get-tuple-element.532, f32[4,512]{1,0:T(4,128)S(1)} %get-tuple-element.533, pred[512,1024]{0,1:T(8,128)(4,1)S(1)} %fusion.67, f32[512,4]{0,1:T(4,128)S(1)} %bitcast.161, bf16[8,1024,128]{1,2,0:T(8,128)(2,1)} %get-tuple-element.554, ...), kind=kOutput, calls=%fused_computation.37.clone.1 | convolution fusion | flops 545783808 | bytes 9716224 | tf_op jit(solution)/shard_map/while/body/eval_jaxpr/rbk,kd->brd/dot_general | solution.py:55
  200.4 6.3 %copy.47 = bf16[512,4096]{1,0:T(8,128)(2,1)} copy(bf16[512,4096]{0,1:T(8,128)(2,1)} %bitcast.23) | data formatting | bytes 8388608 | tf_op jit(solution)/shard_map/reshape | solution.py:69
  207.8 24.0 %while.45 = (s32[]{:T(128)}, f32[32,32]{1,0:T(8,128)S(1)}, f32[32,32]{1,0:T(8,128)S(1)}, f32[32,32,128]{2,1,0:T(8,128)S(1)}, f32[16,32,32]{2,1,0:T(8,128)S(1)}, ...) while((s32[]{:T(128)}, f32[32,32]{1,0:T(8,128)S(1)}, ...), condition=%wide.region_10.11_spmd, body=%wide.region_9.10_spmd.sunk | while | flops 399365 | bytes 1613975 | solution.py:24
  207.8 1.5 fusion.63
  209.4 1.5 fusion.63
  211.0 1.5 fusion.63
  212.6 1.5 fusion.63
  214.2 1.5 fusion.63
  215.8 1.5 fusion.63
  217.4 1.5 fusion.63
  219.0 1.5 fusion.63
  220.6 1.5 fusion.63
  222.2 1.5 fusion.63
  223.8 1.5 fusion.63
  230.2 1.5 fusion.63
  (117 shorter events, 43.7 us)
Async XLA Ops:
  7.2 104.0 %all-reduce.2.cloned.1.call-start = ((), (), s32[]{:S(2)}) async-start(), calls=%async_computation | async-start | bytes 4194304 | tf_op jit(solution)/shard_map/psum | solution.py:14
  11.6 2.0 copy-start
  11.6 195.1 %all-gather.2.cloned.1.call-start = ((), (), s32[]{:S(2)}) async-start(), calls=%async_computation.1 | async-start | bytes 8912896 | tf_op jit(solution)/shard_map/all_gather | solution.py:18
Sparse Core Ops, SparseCore 0:
  11.7 99.4 all-reduce.1
  113.3 72.8 all-gather.1
where the time goes:
time: 244 us; the launch traced here: 239 us
  matrix products  56.9 us (23%)
  other arithmetic  50.5 us (21%)
  waiting for transfers between devices  40.4 us (17%)
  local copies, waits for them, and re-layouts  39.2 us (16%)
  blocking collectives  37 us (15%)
  between operations  14.2 us (6%)
    psum x1, waiting for transfers between devices, from_root(): return lax.psum(jnp.where(mine, x, jnp.zeros_like(x)), axis)  40.4 us
    all_gather x2, blocking collectives, combined_all(): everything = jax.tree.map(lambda part: lax.all_gather(part, axis), x)  37 us
    dot_general x8, matrix products, one_group(): jnp.einsum('rbk,kd->brd', soft_weights, value_part, preferred_element_typ...  27.1 us
    add x15, other arithmetic, combine(): former[2] * factor_former[..., None] + latter[2] * factor_latter[..., None]  23.2 us
    dot_general x8, matrix products, one_group(): jnp.einsum('brd,kd->rbk', query_part, key_part, preferred_element_type=jn...  20.7 us
    reduce_sum x16, other arithmetic, one_group(): totals = jnp.sum(exponent, axis=2)  16.3 us
    unnamed x6, local copies, waits for them, and re-layouts  9.98 us
    dynamic_slice x8, local copies, waits for them, and re-layouts, block_attention(): lax.map(one_group, (group_split(rows_q, groups), group_split(keys_all, gr...  8.76 us
  transfers between devices with their start and end apart: 2, of which 1 were waited for; matrix products, arithmetic and copies ran while one was open for 49% of the time, Pallas kernels for 0%

commit v1 on v0

v1 whole, which is shorter than its diff:
```python
import functools
import math

import jax
import jax.numpy as jnp
from jax import lax
from jax.experimental import pallas as pl
from jax.experimental.pallas import tpu as pltpu
from jax.sharding import PartitionSpec as P

HEAD = 128
UNIT = HEAD ** (-0.5) * math.log2(math.e)
LOW = -1e30
MESH = pl.DeviceIdType.MESH


def chip_width(mesh):
    n = mesh.shape["seq"]
    if n < 8 or n % 4:
        return 1
    try:
        row = mesh.devices.reshape(-1, n)[0]
        a, b, c = row[0].coords, row[2].coords, row[4].coords
    except (AttributeError, TypeError):
        return 1
    return 2 if a[1] != b[1] and a[2] == b[2] and a[2] != c[2] and a[1] == c[1] else 1


def trees(n, width):
    long = n // 2 // width
    dev = lambda z, y, core: (z * width + y) * 2 + core
    streams = []
    for x in (0, 1):
        kids = [[] for _ in range(n)]
        if width == 1:
            if x == 0:
                for z in range(long):
                    if z + 1 < long:
                        kids[dev(z, 0, 0)].append(dev(z + 1, 0, 0))
                    kids[dev(z, 0, 0)].append(dev(z, 0, 1))
            else:
                if long > 1:
                    kids[0].append(dev(1, 0, 1))
                kids[0].append(1)
                for z in range(1, long):
                    if z + 1 < long:
                        kids[dev(z, 0, 1)].append(dev(z + 1, 0, 1))
                    kids[dev(z, 0, 1)].append(dev(z, 0, 0))
        else:
            near, far = (0, 1) if x == 0 else (1, 0)
            if x == 1:
                kids[0].extend((dev(0, 1, 1), 1))
            for z in range(long):
                head = dev(z, near, x)
                if z + 1 < long:
                    kids[head].append(dev(z + 1, near, x))
                if z >= 1:
                    kids[head].append(dev(z, far, x))
                kids[head].append(dev(z, near, 1 - x))
                if z >= 1:
                    kids[dev(z, far, x)].append(dev(z, far, 1 - x))
            if x == 0:
                kids[dev(1, 1, 0)].append(dev(0, 1, 0))
                kids[dev(0, 1, 0)].append(dev(0, 1, 1))
        depth = [0.0] * n
        order = [0]
        for d in order:
            for k in kids[d]:
                depth[k] = depth[d] + (0.5 if k // 2 == d // 2 else 1.0)
                order.append(k)
        assert sorted(order) == list(range(n))
        streams.append((kids, depth))
    return streams


def pick(me, table):
    out = jnp.int32(table[0])
    for i in range(1, len(table)):
        if table[i] != table[0]:
            out = jnp.where(me == i, jnp.int32(table[i]), out)
    return out


def kernel(
    n, plan, groups, ratio,
    q_hbm, kv_hbm, qu_hbm, out_hbm, ans_ref,
    q, own, anc, acc, high, den, outv, qu, stack, qn, qb, st, rb, rst, ans,
    q_sem, own_sem, qu_sem, out_sem, a_send, a_recv, n_send, n_recv, s_send, s_recv,
):
    rows = q.shape[0]
    gw = ratio * HEAD
    me = lax.axis_index("seq")
    kid_max = max(len(k) for kids, _ in plan for k in kids)

    barrier = pltpu.get_barrier_semaphore()

    def greet(k, c):
        pl.semaphore_signal(
            barrier, inc=1, device_id={"seq": lax.rem(me + k, n)}, device_id_type=MESH
        )
        return c

    lax.fori_loop(1, n, greet, 0)

    def own_copy(kind, g):
        return pltpu.make_async_copy(
            kv_hbm.at[kind, :, pl.ds(pl.multiple_of(g * HEAD, HEAD), HEAD)],
            own.at[kind * groups + g],
            own_sem.at[kind * groups + g],
        )

    def q_copy(g):
        cols = pl.ds(pl.multiple_of(g * gw, gw), gw)
        return pltpu.make_async_copy(q_hbm.at[:, cols], q.at[:, cols], q_sem.at[g])

    def out_copy(g):
        cols = pl.ds(pl.multiple_of(g * gw, gw), gw)
        return pltpu.make_async_copy(outv.at[:, cols], out_hbm.at[:, cols], out_sem.at[g])

    qu_copy = pltpu.make_async_copy(qu_hbm, qu, qu_sem)
    for g in range(groups):
        own_copy(0, g).start()
        own_copy(1, g).start()
        q_copy(g).start()
    qu_copy.start()

    kids_of = []
    depth_of = []
    for kids, depth in plan:
        padded = [k + [-1] * (kid_max - len(k)) for k in kids]
        kids_of.append([pick(me, [p[j] for p in padded]) for j in range(kid_max)])
        depth_of.append(pick(me, [2 + int(4 * max(d - 1, 0)) for d in depth]))

    pl.semaphore_wait(barrier, n - 1)

    per = groups

    def piece(x, k):
        g = (k // 2) * 2 + x
        kind = lax.rem(k, 2)
        return kind, g, kind * groups + g

    @pl.when(me == 0)
    def _():
        def inject(k, c):
            for x in (0, 1):
                kind, g, idx = piece(x, k)
                for j, kid in enumerate(plan[x][0][0]):
                    pltpu.make_async_remote_copy(
                        src_ref=kv_hbm.at[kind, :, pl.ds(pl.multiple_of(g * HEAD, HEAD), HEAD)],
                        dst_ref=anc.at[idx],
                        send_sem=a_send.at[idx, j],
                        recv_sem=a_recv.at[idx],
                        device_id={"seq": kid},
                        device_id_type=MESH,
                    ).start()
            return c

        lax.fori_loop(0, per, inject, 0)

    def hop(idx, j, kid):
        return pltpu.make_async_remote_copy(
            src_ref=anc.at[idx],
            dst_ref=anc.at[idx],
            send_sem=a_send.at[idx, j],
            recv_sem=a_recv.at[idx],
            device_id={"seq": kid},
            device_id_type=MESH,
        )

    def serve(x, k):
        _, _, idx = piece(x, k)
        hop(idx, 0, jnp.int32(0)).wait_recv()
        for j in range(kid_max):
            kid = kids_of[x][j]

            @pl.when(kid >= 0)
            def _():
                hop(idx, j, kid).start()

    def due(x, slot):
        return jnp.clip((slot - depth_of[x]) // 2, 0, per)

    def serve_range(x, lo, hi):
        @pl.when(me > 0)
        def _():
            lax.fori_loop(lo, hi, lambda k, c: (serve(x, k), c)[1], 0)

    cdims = (((1,), (1,)), ((), ()))
    ones = jnp.ones((rows, HEAD), jnp.bfloat16)
    rb_rows = min(rows, 256)
    pairs = ratio // 2 if ratio % 2 == 0 else ratio
    heads_per = ratio // pairs
    steps = groups * pairs

    def local_step(i, c):
        g = i // pairs
        for x in (0, 1):
            serve_range(x, due(x, i - 1), due(x, i))

        @pl.when(lax.rem(i, pairs) == 0)
        def _():
            own_copy(0, g).wait()
            own_copy(1, g).wait()
            q_copy(g).wait()

        for h in range(heads_per):
            cols = pl.ds(pl.multiple_of((i * heads_per + h) * HEAD, HEAD), HEAD)
            for r0 in range(0, rows, rb_rows):
                rs = pl.ds(r0, rb_rows)
                qt = q[rs, cols]
                key = own[g, pl.ds(0, r0 + rb_rows), :]
                val = own[groups + g, pl.ds(0, r0 + rb_rows), :]
                s = lax.dot_general(qt, key, cdims, preferred_element_type=jnp.float32)
                row_pos = lax.broadcasted_iota(jnp.int32, (rb_rows, rb_rows), 0)
                col_pos = lax.broadcasted_iota(jnp.int32, (rb_rows, rb_rows), 1)
                last = jnp.where(col_pos <= row_pos, s[:, r0:], LOW)
                s = jnp.concatenate((s[:, :r0], last), axis=1) if r0 else last
                m = jnp.max(s, axis=1, keepdims=True)
                p = jnp.exp2((s - m) * UNIT).astype(jnp.bfloat16)
                wide = jnp.concatenate((val, ones[: r0 + rb_rows]), axis=1)
                o = lax.dot(p, wide, preferred_element_type=jnp.float32)
                acc[rs, cols] = o[:, :HEAD]
                den[rs, cols] = o[:, HEAD:]
                high[rs, cols] = jnp.broadcast_to(m, (rb_rows, HEAD))
        return c

    lax.fori_loop(0, steps, local_step, 0)

    qu_copy.wait()
    qrows = qu.shape[0]
    share = qrows // n
    rr = share * ratio

    def question_step(g, c):
        mm, dd = c
        for h in range(ratio):
            cols = pl.ds(pl.multiple_of((g * ratio + h) * HEAD, HEAD), HEAD)
            stack[pl.ds(h, qrows, stride=ratio), :] = qu[:, cols].astype(jnp.float32)
        qt = stack[...].astype(jnp.bfloat16)
        s = lax.dot_general(qt, own[g], cdims, preferred_element_type=jnp.float32)
        m = jnp.max(s, axis=1, keepdims=True)
        p = jnp.exp2((s - m) * UNIT).astype(jnp.bfloat16)
        wide = jnp.concatenate((own[groups + g], ones), axis=1)
        o = lax.dot(p, wide, preferred_element_type=jnp.float32)
        qn[:, g] = o[:, :HEAD].reshape(n, rr, HEAD)
        lane = lax.broadcasted_iota(jnp.int32, (qrows * ratio, HEAD), 1)
        mm = jnp.where(lane == g, m, mm)
        dd = jnp.where(lane == g, o[:, HEAD:], dd)
        return mm, dd

    zero = jnp.zeros((qrows * ratio, HEAD), jnp.float32)
    mm, dd = lax.fori_loop(0, groups, question_step, (zero, zero))
    st[:, 0] = mm.reshape(n, rr, HEAD)
    st[:, 1] = dd.reshape(n, rr, HEAD)

    def narrow(i, c):
        qb[i] = qn[i].reshape(groups * rr, HEAD).astype(jnp.bfloat16)
        return c

    lax.fori_loop(0, n, narrow, 0)

    def exchange(k):
        to = lax.rem(me + k, n)
        return (
            pltpu.make_async_remote_copy(
                src_ref=qb.at[to], dst_ref=rb.at[me], send_sem=n_send.at[to],
                recv_sem=n_recv.at[me], device_id={"seq": to}, device_id_type=MESH,
            ),
            pltpu.make_async_remote_copy(
                src_ref=st.at[to], dst_ref=rst.at[me], send_sem=s_send.at[to],
                recv_sem=s_recv.at[me], device_id={"seq": to}, device_id_type=MESH,
            ),
        )

    def arrived(k):
        frm = lax.rem(me + n - k, n)
        to = lax.rem(me + k, n)
        return (
            pltpu.make_async_remote_copy(
                src_ref=qb.at[to], dst_ref=rb.at[frm], send_sem=n_send.at[to],
                recv_sem=n_recv.at[frm], device_id={"seq": to}, device_id_type=MESH,
            ),
            pltpu.make_async_remote_copy(
                src_ref=st.at[to], dst_ref=rst.at[frm], send_sem=s_send.at[to],
                recv_sem=s_recv.at[frm], device_id={"seq": to}, device_id_type=MESH,
            ),
        )

    def anchor_step(i, c):
        slot = i + steps
        g = i // pairs

        def upto(x, j):
            jg = j // pairs
            asked = jnp.where(j < 0, 0, ((jg + 2 - x) // 2) * 2)
            return jnp.maximum(due(x, j + steps), asked)

        for x in (0, 1):
            serve_range(x, upto(x, i - 1), upto(x, i))

        @pl.when(i == 1)
        def _():
            def go(k, c):
                for copy in exchange(k):
                    copy.start()
                return c

            lax.fori_loop(1, n, go, 0)

        @pl.when(me == 0)
        def _():
            for h in range(heads_per):
                cols = pl.ds(pl.multiple_of((i * heads_per + h) * HEAD, HEAD), HEAD)
                outv[:, cols] = (acc[:, cols] / den[:, cols]).astype(jnp.bfloat16)

        @pl.when(me > 0)
        def _():
            for h in range(heads_per):
                cols = pl.ds(pl.multiple_of((i * heads_per + h) * HEAD, HEAD), HEAD)
                for r0 in range(0, rows, rb_rows):
                    rs = pl.ds(r0, rb_rows)
                    s = lax.dot_general(
                        q[rs, cols], anc[g], cdims, preferred_element_type=jnp.float32
                    )
                    ml = high[rs, cols]
                    m = jnp.maximum(jnp.max(s, axis=1, keepdims=True), ml)
                    mw = jnp.concatenate([m] * (s.shape[1] // HEAD), axis=1)
                    p = jnp.exp2((s - mw) * UNIT).astype(jnp.bfloat16)
                    wide = jnp.concatenate((anc[groups + g], ones), axis=1)
                    o = lax.dot(p, wide, preferred_element_type=jnp.float32)
                    f = jnp.exp2((ml - m) * UNIT)
                    num = o[:, :HEAD] + f * acc[rs, cols]
                    total = o[:, HEAD:] + f * den[rs, cols]
                    outv[rs, cols] = (num / total).astype(jnp.bfloat16)

        @pl.when(lax.rem(i, pairs) == pairs - 1)
        def _():
            out_copy(g).start()

        return c

    lax.fori_loop(0, steps, anchor_step, 0)

    rb[me] = qb[me]
    rst[me] = st[me]

    def land(k, c):
        for copy in arrived(k):
            copy.wait()
        return c

    lax.fori_loop(1, n, land, 0)

    top = lax.fori_loop(1, n, lambda j, t: jnp.maximum(t, rst[j, 0]), rst[0, 0])

    def gather(j, c):
        total, nums = c
        w = jnp.exp2((rst[j, 0] - top) * UNIT)
        total = total + w * rst[j, 1]
        part = rb[j].astype(jnp.float32)
        nums = tuple(
            nums[g] + w[:, g : g + 1] * part[g * rr : (g + 1) * rr] for g in range(groups)
        )
        return total, nums

    tile = jnp.zeros((rr, HEAD), jnp.float32)
    total, nums = lax.fori_loop(0, n, gather, (tile, (tile,) * groups))
    for g in range(groups):
        mine = nums[g] / total[:, g : g + 1]
        for r in range(share):
            for h in range(ratio):
                k = r * ratio + h
                ans[r : r + 1, (g * ratio + h) * HEAD : (g * ratio + h + 1) * HEAD] = mine[k : k + 1]
    ans_ref[...] = ans[...].astype(jnp.bfloat16)

    def sent(idx, c):
        g = lax.rem(idx, groups)
        for x in (0, 1):
            for j in range(kid_max):

                @pl.when((lax.rem(g, 2) == x) & (kids_of[x][j] >= 0))
                def _():
                    hop(idx, j, jnp.maximum(kids_of[x][j], 0)).wait_send()

        return c

    lax.fori_loop(0, 2 * groups, sent, 0)
    for g in range(groups):
        out_copy(g).wait()


def solution(mesh):
    n = mesh.shape["seq"]
    plan = trees(n, chip_width(mesh))
    kid_max = max(len(k) for kids, _ in plan for k in kids)

    def on_device(queries, kv_cache, question):
        rows, width = queries.shape
        groups = kv_cache.shape[2] // HEAD
        ratio = width // kv_cache.shape[2]
        qrows = question.shape[0]
        share = qrows // n
        rr = share * ratio
        any_space = pl.BlockSpec(memory_space=pl.ANY)
        dma = pltpu.SemaphoreType.DMA
        return pl.pallas_call(
            functools.partial(kernel, n, plan, groups, ratio),
            out_shape=(
                jax.ShapeDtypeStruct((rows, width), jnp.bfloat16),
                jax.ShapeDtypeStruct((share, width), jnp.bfloat16),
            ),
            in_specs=[any_space] * 3,
            out_specs=(any_space, pl.BlockSpec(memory_space=pltpu.VMEM)),
            scratch_shapes=[
                pltpu.VMEM((rows, width), jnp.bfloat16),
                pltpu.VMEM((2 * groups, rows, HEAD), jnp.bfloat16),
                pltpu.VMEM((2 * groups, rows, HEAD), jnp.bfloat16),
                pltpu.VMEM((rows, width), jnp.float32),
                pltpu.VMEM((rows, width), jnp.float32),
                pltpu.VMEM((rows, width), jnp.float32),
                pltpu.VMEM((rows, width), jnp.bfloat16),
                pltpu.VMEM((qrows, width), jnp.bfloat16),
                pltpu.VMEM((qrows * ratio, HEAD), jnp.float32),
                pltpu.VMEM((n, groups, rr, HEAD), jnp.float32),
                pltpu.VMEM((n, groups * rr, HEAD), jnp.bfloat16),
                pltpu.VMEM((n, 2, rr, HEAD), jnp.float32),
                pltpu.VMEM((n, groups * rr, HEAD), jnp.bfloat16),
                pltpu.VMEM((n, 2, rr, HEAD), jnp.float32),
                pltpu.VMEM((share, width), jnp.float32),
                dma((groups,)),
                dma((2 * groups,)),
                dma,
                dma((groups,)),
                dma((2 * groups, kid_max)),
                dma((2 * groups,)),
                dma((n,)),
                dma((n,)),
                dma((n,)),
                dma((n,)),
            ],
            compiler_params=pltpu.CompilerParams(
                collective_id=0, has_side_effects=True, vmem_limit_bytes=56 * 2**20
            ),
        )(queries, kv_cache, question)

    return jax.shard_map(
        on_device,
        mesh=mesh,
        in_specs=(P(("grp", "seq"), None), P(None, ("grp", "seq"), None), P("grp", None)),
        out_specs=(P(("grp", "seq"), None), P(("grp", "seq"), None)),
        check_vma=False,
    )
```

time: 244 us -> 71.4 us (0.29); the launches traced: 239 us -> 71.2 us
  Pallas kernels: 0 us -> 65.2 us
  matrix products: 56.9 us -> 0 us
  other arithmetic: 50.5 us -> 0 us
  waiting for transfers between devices: 40.4 us -> 0 us
  blocking collectives: 37 us -> 0 us
  local copies, waits for them, and re-layouts: 39.2 us -> 5.31 us
  between operations: 14.2 us -> 0.65 us
    pallas_call x0 -> x1, Pallas kernels: none -> 65.2 us  [on_device(): pl.pallas_call(functools.partial(kernel, n, plan, groups, ratio), out_sha...]
    dot_general x32 -> x0, matrix products: 56.9 us -> none  [the longest x8 27.1 us: one_group(): jnp.einsum('rbk,kd->brd', soft_weights, value_part, preferred_element_typ...]
    psum x1 -> x0, waiting for transfers between devices: 40.4 us -> none  [from_root(): return lax.psum(jnp.where(mine, x, jnp.zeros_like(x)), axis)]
    all_gather x2 -> x0, blocking collectives: 37 us -> none  [combined_all(): everything = jax.tree.map(lambda part: lax.all_gather(part, axis), x)]
    add x30 -> x0, other arithmetic: 23.5 us -> none  [the longest x15 23.2 us: combine(): former[2] * factor_former[..., None] + latter[2] * factor_latter[..., None]]
    reduce_sum x16 -> x0, other arithmetic: 16.3 us -> none  [one_group(): totals = jnp.sum(exponent, axis=2)]
    dynamic_slice x17 -> x0, local copies, waits for them, and re-layouts: 8.84 us -> none  [the longest x8 8.76 us: block_attention(): lax.map(one_group, (group_split(rows_q, groups), group_split(keys_all, gr...]
    select_n x9 -> x0, other arithmetic: 8.14 us -> none  [the longest x8 6.68 us: visible(): jnp.where(column < anchor_rows, block_number > 0, column - anchor_rows <=...]
  transfers between devices with their start and end apart: 2 -> 0, of which waited for: 1 -> 0; matrix products, arithmetic and copies ran while one was open for 49% -> 0% of each run, Pallas kernels for 0% -> 0%
where the time goes in v1:
time: 71.4 us; the launch traced here: 71.2 us
  Pallas kernels  65.2 us (91%)
  local copies, waits for them, and re-layouts  5.31 us (7%)
    pallas_call x1, Pallas kernels, on_device(): pl.pallas_call(functools.partial(kernel, n, plan, groups, ratio), out_sha...  65.2 us
    unnamed x4, local copies, waits for them, and re-layouts  5.31 us

profile of v1, /device:TPU:24, one launch (start us, length us, event | category | flops | bytes accessed | tf_op | source)
XLA Modules:
  0.0 71.2 jit_solution(4216032684386266468)
XLA Ops:
  0.6 65.2 %shard_map.50 = (bf16[512,4096]{1,0:T(8,128)(2,1)}, bf16[2,4096]{1,0:T(2,128)(2,1)}) custom-call(bf16[512,4096]{1,0:T(8,128)(2,1)} %q_hbm.1, bf16[2,512,1024]{2,1,0:T(8,128)(2,1)} %kv_hbm.1, bf16[32,4096]{1,0:T(8,128)(2,1)} %qu_hbm.1), custom_call_target="tpu_custom_call" | custom-call | tf_op jit(solution)/shard_map/pallas_call | solution.py:407
  65.9 0.0 copy-start
  65.9 4.7 %copy.7 = bf16[512,4096]{1,0:T(8,128)(2,1)} copy(bf16[512,4096]{1,0:T(8,128)(2,1)} %get-tuple-element.4) | data formatting | bytes 8388608
  70.6 0.0 copy-done
  70.6 0.6 copy.8
Async XLA Ops:
  65.9 4.7 %copy-start = (bf16[2,4096]{1,0:T(2,128)(2,1)S(1)}, bf16[2,4096]{1,0:T(2,128)(2,1)}, u32[]{:S(2)}) copy-start(bf16[2,4096]{1,0:T(2,128)(2,1)} %get-tuple-element.5) | copy-start | bytes 49156

commit v2 on v1

--- a/solution.py
+++ b/solution.py
@@ -118,18 +118,19 @@
         return pltpu.make_async_copy(outv.at[:, cols], out_hbm.at[:, cols], out_sem.at[g])
 
     qu_copy = pltpu.make_async_copy(qu_hbm, qu, qu_sem)
+    qu_copy.start()
     for g in range(groups):
         own_copy(0, g).start()
         own_copy(1, g).start()
+    for g in range(groups):
         q_copy(g).start()
-    qu_copy.start()
 
     kids_of = []
     depth_of = []
     for kids, depth in plan:
         padded = [k + [-1] * (kid_max - len(k)) for k in kids]
         kids_of.append([pick(me, [p[j] for p in padded]) for j in range(kid_max)])
-        depth_of.append(pick(me, [2 + int(4 * max(d - 1, 0)) for d in depth]))
+        depth_of.append(pick(me, [int(2 * max(d - 1, 0)) for d in depth]))
 
     pl.semaphore_wait(barrier, n - 1)
 
@@ -179,7 +180,8 @@
                 hop(idx, j, kid).start()
 
     def due(x, slot):
-        return jnp.clip((slot - depth_of[x]) // 2, 0, per)
+        late = slot - depth_of[x]
+        return jnp.where(late < 0, 0, jnp.minimum((late * 6 + 9) // 5, per))
 
     def serve_range(x, lo, hi):
         @pl.when(me > 0)
@@ -189,9 +191,45 @@
     cdims = (((1,), (1,)), ((), ()))
     ones = jnp.ones((rows, HEAD), jnp.bfloat16)
     rb_rows = min(rows, 256)
-    pairs = ratio // 2 if ratio % 2 == 0 else ratio
-    heads_per = ratio // pairs
-    steps = groups * pairs
+    pairs = 1
+    heads_per = ratio
+    steps = groups
+
+    qu_copy.wait()
+    for g in range(groups):
+        own_copy(0, g).wait()
+        own_copy(1, g).wait()
+    qrows = qu.shape[0]
+    share = qrows // n
+    rr = share * ratio
+
+    def question_step(g, c):
+        mm, dd = c
+        for h in range(ratio):
+            cols = pl.ds(pl.multiple_of((g * ratio + h) * HEAD, HEAD), HEAD)
+            stack[lax.rem(g, 4), pl.ds(h, qrows, stride=ratio), :] = qu[:, cols].astype(jnp.float32)
+        qt = stack[lax.rem(g, 4)].astype(jnp.bfloat16)
+        s = lax.dot_general(qt, own[g], cdims, preferred_element_type=jnp.float32)
+        m = jnp.max(s, axis=1, keepdims=True)
+        p = jnp.exp2((s - m) * UNIT).astype(jnp.bfloat16)
+        wide = jnp.concatenate((own[groups + g], ones), axis=1)
+        o = lax.dot(p, wide, preferred_element_type=jnp.float32)
+        qn[:, g] = o[:, :HEAD].reshape(n, rr, HEAD)
+        lane = lax.broadcasted_iota(jnp.int32, (qrows * ratio, HEAD), 1)
+        mm = jnp.where(lane == g, m, mm)
+        dd = jnp.where(lane == g, o[:, HEAD:], dd)
+        return mm, dd
+
+    zero = jnp.zeros((qrows * ratio, HEAD), jnp.float32)
+    mm, dd = lax.fori_loop(0, groups, question_step, (zero, zero), unroll=4)
+    st[:, 0] = mm.reshape(n, rr, HEAD)
+    st[:, 1] = dd.reshape(n, rr, HEAD)
+
+    def narrow(i, c):
+        qb[i] = qn[i].reshape(groups * rr, HEAD).astype(jnp.bfloat16)
+        return c
+
+    lax.fori_loop(0, n, narrow, 0, unroll=4)
 
     def local_step(i, c):
         g = i // pairs
@@ -200,8 +238,6 @@
 
         @pl.when(lax.rem(i, pairs) == 0)
         def _():
-            own_copy(0, g).wait()
-            own_copy(1, g).wait()
             q_copy(g).wait()
 
         for h in range(heads_per):
@@ -227,39 +263,6 @@
 
     lax.fori_loop(0, steps, local_step, 0)
 
-    qu_copy.wait()
-    qrows = qu.shape[0]
-    share = qrows // n
-    rr = share * ratio
-
-    def question_step(g, c):
-        mm, dd = c
-        for h in range(ratio):
-            cols = pl.ds(pl.multiple_of((g * ratio + h) * HEAD, HEAD), HEAD)
-            stack[pl.ds(h, qrows, stride=ratio), :] = qu[:, cols].astype(jnp.float32)
-        qt = stack[...].astype(jnp.bfloat16)
-        s = lax.dot_general(qt, own[g], cdims, preferred_element_type=jnp.float32)
-        m = jnp.max(s, axis=1, keepdims=True)
-        p = jnp.exp2((s - m) * UNIT).astype(jnp.bfloat16)
-        wide = jnp.concatenate((own[groups + g], ones), axis=1)
-        o = lax.dot(p, wide, preferred_element_type=jnp.float32)
-        qn[:, g] = o[:, :HEAD].reshape(n, rr, HEAD)
-        lane = lax.broadcasted_iota(jnp.int32, (qrows * ratio, HEAD), 1)
-        mm = jnp.where(lane == g, m, mm)
-        dd = jnp.where(lane == g, o[:, HEAD:], dd)
-        return mm, dd
-
-    zero = jnp.zeros((qrows * ratio, HEAD), jnp.float32)
-    mm, dd = lax.fori_loop(0, groups, question_step, (zero, zero))
-    st[:, 0] = mm.reshape(n, rr, HEAD)
-    st[:, 1] = dd.reshape(n, rr, HEAD)
-
-    def narrow(i, c):
-        qb[i] = qn[i].reshape(groups * rr, HEAD).astype(jnp.bfloat16)
-        return c
-
-    lax.fori_loop(0, n, narrow, 0)
-
     def exchange(k):
         to = lax.rem(me + k, n)
         return (
@@ -299,7 +302,7 @@
         for x in (0, 1):
             serve_range(x, upto(x, i - 1), upto(x, i))
 
-        @pl.when(i == 1)
+        @pl.when(i == 2)
         def _():
             def go(k, c):
                 for copy in exchange(k):
@@ -365,7 +368,7 @@
         return total, nums
 
     tile = jnp.zeros((rr, HEAD), jnp.float32)
-    total, nums = lax.fori_loop(0, n, gather, (tile, (tile,) * groups))
+    total, nums = lax.fori_loop(0, n, gather, (tile, (tile,) * groups), unroll=2)
     for g in range(groups):
         mine = nums[g] / total[:, g : g + 1]
         for r in range(share):
@@ -421,7 +424,7 @@
                 pltpu.VMEM((rows, width), jnp.float32),
                 pltpu.VMEM((rows, width), jnp.bfloat16),
                 pltpu.VMEM((qrows, width), jnp.bfloat16),
-                pltpu.VMEM((qrows * ratio, HEAD), jnp.float32),
+                pltpu.VMEM((4, qrows * ratio, HEAD), jnp.float32),
                 pltpu.VMEM((n, groups, rr, HEAD), jnp.float32),
                 pltpu.VMEM((n, groups * rr, HEAD), jnp.bfloat16),
                 pltpu.VMEM((n, 2, rr, HEAD), jnp.float32),

time: 71.4 us -> 51.9 us (0.73)
  the two profiles are of different devices: /device:TPU:24 before, /device:TPU:19 now
where the time goes in v2:
time: 51.9 us; the launch traced here: 51.7 us
  Pallas kernels  45.8 us (88%)
  local copies, waits for them, and re-layouts  5.31 us (10%)
  between operations  0.65 us (1%)
    pallas_call x1, Pallas kernels, on_device(): pl.pallas_call(functools.partial(kernel, n, plan, groups, ratio), out_sha...  45.8 us
    unnamed x4, local copies, waits for them, and re-layouts  5.31 us

profile of v2, /device:TPU:19, one launch (start us, length us, event | category | flops | bytes accessed | tf_op | source)
XLA Modules:
  0.0 51.7 jit_solution(6911152894854061356)
XLA Ops:
  0.6 45.8 %shard_map.50 = (bf16[512,4096]{1,0:T(8,128)(2,1)}, bf16[2,4096]{1,0:T(2,128)(2,1)}) custom-call(bf16[512,4096]{1,0:T(8,128)(2,1)} %q_hbm.1, bf16[2,512,1024]{2,1,0:T(8,128)(2,1)} %kv_hbm.1, bf16[32,4096]{1,0:T(8,128)(2,1)} %qu_hbm.1), custom_call_target="tpu_custom_call" | custom-call | tf_op jit(solution)/shard_map/pallas_call | solution.py:410
  46.4 0.0 copy-start
  46.4 4.7 %copy.7 = bf16[512,4096]{1,0:T(8,128)(2,1)} copy(bf16[512,4096]{1,0:T(8,128)(2,1)} %get-tuple-element.4) | data formatting | bytes 8388608
  51.1 0.0 copy-done
  51.1 0.6 %copy.8 = bf16[2,4096]{1,0:T(2,128)(2,1)} copy(bf16[2,4096]{1,0:T(2,128)(2,1)S(1)} %copy-done) | data formatting | bytes 32768
Async XLA Ops:
  46.4 4.7 %copy-start = (bf16[2,4096]{1,0:T(2,128)(2,1)S(1)}, bf16[2,4096]{1,0:T(2,128)(2,1)}, u32[]{:S(2)}) copy-start(bf16[2,4096]{1,0:T(2,128)(2,1)} %get-tuple-element.5) | copy-start | bytes 49156
